TPU v7x, 32 devices: a whole 2x2x4 slice. The times are simulated.
32 devices in a mesh: groups: 2 (over y), seq: 16 (over z, x, core).
Axes of the slice: x: 2, y: 2, z: 4, core: 2. Of those that a mesh axis runs over, the one named last changes fastest.
Arguments:
- queries: bfloat16 [8192, 2048], P(('groups', 'seq')), parts along dimension 0, may hold values from -20 to 20
- keys: bfloat16 [8192, 2048], P(('groups', 'seq')), parts along dimension 0, may hold values from -20 to 20
- values: bfloat16 [8192, 2048], P(('groups', 'seq')), parts along dimension 0, may hold values from -6 to 6
- block_counts: int32 [16], P('groups'), parts along dimension 0, may hold values from 2 to 6, as said below
- last_tokens: int32 [32], P('groups'), parts along dimension 0, may hold values from 64 to 128
- pack_order: int32 [32], P('groups'), parts along dimension 0, may hold values from 0 to 15, as said below
- decode_slot: int32 [16], P('groups'), parts along dimension 0, may hold values from 0 to 7, each once
Outputs:
- attended: bfloat16 [8192, 2048], P(('groups', 'seq')), parts along dimension 0
- cache_keys: bfloat16 [32, 32, 128, 128], P(('groups', 'seq')), parts along dimension 0
- cache_values: bfloat16 [32, 32, 128, 128], P(('groups', 'seq')), parts along dimension 0
There are 2 independent parts, one for each index of `groups`. A program takes and returns all parts, laid end to end along the dimension named above; each array names one. Nothing has to cross between parts.
Inputs may be any that keep to these rules, and one draw needn't show every extreme that they name: `block_counts`: they sum to 24; the largest equals 6. `pack_order`: each prompt number appears once. The last 1 positions hold null prompts, and the position before them a conditional prompt of 6 blocks. `decode_slot`: each slot appears once.
All inputs are finite; a program needn't handle non-finite values.
Results may differ from a plain program's by a relative error of at most 0.0034.
Values may be sent and summed in bfloat16 or wider, within the bound.
No kernel may reach another device: no remote copies, remote signals or barrier semaphores. Data moves between devices by JAX's collectives and lax.ppermute only.
A program may use at most 64 MiB of HBM per device.

v0:
```python
import jax
import jax.numpy as jnp
from jax import lax
from jax.sharding import PartitionSpec as P

HEADS = 16
HEAD_DIM = 128
BLOCK = 128
MAXB = 6


MASKED_SCORE = -1e30


def shifted(block, axis, distance):
    devices = range(lax.axis_size(axis))
    route = [(i - distance, i) for i in devices if i - distance in devices]
    return lax.ppermute(block, axis, route)


def block_tables(block_counts, last_tokens, pack_order, decode_slot, total_blocks, block):
    pair_count = block_counts.shape[0]
    prompts = 2 * pair_count
    prompt_ids = jnp.arange(prompts, dtype=jnp.int32)
    prompt_sizes = jnp.concatenate([block_counts, jnp.ones((pair_count,), jnp.int32)])
    picked = (pack_order[:, None] == prompt_ids[None, :]).astype(jnp.int32)
    packed_sizes = jnp.sum(picked * prompt_sizes[None, :], axis=1)
    packed_tails = jnp.sum(picked * last_tokens[None, :], axis=1)
    block_ends = jnp.cumsum(packed_sizes)
    starts = block_ends - packed_sizes
    blocks = jnp.arange(total_blocks, dtype=jnp.int32)
    member = (
        (starts[None, :] <= blocks[:, None]) & (blocks[:, None] < block_ends[None, :])
    ).astype(jnp.int32)
    position = jnp.sum(member * prompt_ids[None, :], axis=1)
    prompt = jnp.sum(member * pack_order[None, :], axis=1)
    within = blocks - jnp.sum(member * starts[None, :], axis=1)
    is_last = blocks + 1 == jnp.sum(member * block_ends[None, :], axis=1)
    valid_tokens = jnp.where(is_last, jnp.sum(member * packed_tails[None, :], axis=1), block)
    pair_ids = jnp.arange(pair_count, dtype=jnp.int32)
    earlier = (decode_slot[None, :] < decode_slot[:, None]).astype(jnp.int32)
    slot_start = jnp.sum(earlier * (block_counts + 1)[None, :], axis=1)
    pair_of = prompt % pair_count
    owner = (pair_of[:, None] == pair_ids[None, :]).astype(jnp.int32)
    base_slot = jnp.sum(owner * slot_start[None, :], axis=1)
    own_count = jnp.sum(owner * block_counts[None, :], axis=1)
    destination = base_slot + jnp.where(prompt >= pair_count, own_count, within)
    hits = (destination[None, :] == blocks[:, None]).astype(jnp.int32)
    source = jnp.sum(hits * blocks[None, :], axis=1)
    return (position, valid_tokens, source)


def hand_off(paired, source, devices):
    tokens_here = paired.shape[1]
    blocks_here = tokens_here // BLOCK
    splits = devices // HEADS
    slice_len = BLOCK // splits
    outgoing = paired.reshape(2, blocks_here, splits, slice_len, HEADS, HEAD_DIM)
    outgoing = jnp.transpose(outgoing, (4, 2, 0, 1, 3, 5)).reshape(
        devices, 2, blocks_here, slice_len, HEAD_DIM
    )
    arrived = lax.all_to_all(outgoing, "seq", split_axis=0, concat_axis=2, tiled=True)
    ordered = jnp.take(arrived[0], source, axis=1)
    return (ordered[0][None], ordered[1][None])


def attend(queries, paired, position, valid_tokens, own_index, reach):
    tokens_here, features = queries.shape
    blocks_here = tokens_here // BLOCK
    pieces = [paired]
    current = paired
    for distance in range(reach):
        current = shifted(current, "seq", 1)
        pieces.insert(0, current)
    prior_count = reach * blocks_here
    window = jnp.concatenate(pieces, axis=1)
    window_blocks = prior_count + blocks_here
    lead_blocks = reach * blocks_here
    padded_docs = jnp.concatenate([jnp.full((lead_blocks,), -1, jnp.int32), position])
    padded_valid = jnp.concatenate([jnp.zeros((lead_blocks,), jnp.int32), valid_tokens])
    first_block = own_index * blocks_here + lead_blocks - prior_count
    window_docs = lax.dynamic_slice_in_dim(padded_docs, first_block, window_blocks)
    window_valid = lax.dynamic_slice_in_dim(padded_valid, first_block, window_blocks)
    own_first = own_index * blocks_here
    query_docs = lax.dynamic_slice_in_dim(position, own_first, blocks_here)
    query_valid = lax.dynamic_slice_in_dim(valid_tokens, own_first, blocks_here)
    token_ids = jnp.arange(BLOCK, dtype=jnp.int32)
    key_docs = jnp.repeat(window_docs, BLOCK)
    key_limit = jnp.repeat(window_valid, BLOCK)
    key_tokens = jnp.tile(token_ids, window_blocks)
    key_order = jnp.arange(window_blocks * BLOCK, dtype=jnp.int32) - prior_count * BLOCK
    query_order = jnp.arange(tokens_here, dtype=jnp.int32)
    allowed = key_docs[None, :] == jnp.repeat(query_docs, BLOCK)[:, None]
    allowed = (
        allowed & (key_order[None, :] <= query_order[:, None]) & (key_tokens < key_limit)[None, :]
    )
    query_ok = jnp.tile(token_ids, blocks_here) < jnp.repeat(query_valid, BLOCK)
    score_scale = HEAD_DIM ** (-0.5)
    query_heads = jnp.moveaxis(queries.reshape(tokens_here, HEADS, HEAD_DIM), 1, 0)
    key_heads = jnp.moveaxis(window[0].reshape(-1, HEADS, HEAD_DIM), 1, 0)
    value_heads = jnp.moveaxis(window[1].reshape(-1, HEADS, HEAD_DIM), 1, 0)

    def one_head(operands):
        query_part, key_part, value_part = operands
        scores = (
            jnp.einsum("qd,kd->qk", query_part, key_part, preferred_element_type=jnp.float32)
            * score_scale
        )
        scores = jnp.where(allowed, scores, MASKED_SCORE)
        peak = jnp.max(scores, axis=1, keepdims=True)
        weights = jnp.exp(scores - peak)
        totals = jnp.sum(weights, axis=1, keepdims=True)
        mixed = jnp.dot(
            weights.astype(jnp.bfloat16), value_part, preferred_element_type=jnp.float32
        )
        return mixed / totals

    head_outputs = lax.map(one_head, (query_heads, key_heads, value_heads))
    merged = jnp.moveaxis(head_outputs, 0, 1).reshape(tokens_here, features)
    return jnp.where(query_ok[:, None], merged, 0.0).astype(jnp.bfloat16)


def local(queries, keys, values, block_counts, last_tokens, pack_order, decode_slot):
    devices = lax.axis_size("seq")
    own_index = lax.axis_index("seq")
    tokens_here = queries.shape[0]
    blocks_here = tokens_here // BLOCK
    reach = (MAXB + blocks_here - 2) // blocks_here
    position, valid_tokens, source = block_tables(
        block_counts, last_tokens, pack_order, decode_slot, blocks_here * devices, BLOCK
    )
    paired = jnp.stack([keys, values])
    attended = attend(queries, paired, position, valid_tokens, own_index, reach)
    cache_keys, cache_values = hand_off(paired, source, devices)
    return (attended, cache_keys, cache_values)


def solution(mesh):
    placed = (
        P(("groups", "seq"), None),
        P(("groups", "seq"), None),
        P(("groups", "seq"), None),
        P("groups"),
        P("groups"),
        P("groups"),
        P("groups"),
    )
    return jax.shard_map(
        local,
        mesh=mesh,
        in_specs=placed,
        out_specs=(
            P(("groups", "seq"), None),
            P(("groups", "seq"), None, None, None),
            P(("groups", "seq"), None, None, None),
        ),
        check_vma=False,
    )
```

profile of v0, /device:TPU:20, one launch (start us, length us, event | category | flops | bytes accessed | tf_op | source)
XLA Modules:
  0.0 189.0 jit_solution(15952049757768567406)
XLA Ops:
  0.6 1.6 copy.47
  2.8 1.5 pad_maximum_fusion
  4.2 1.9 %collective-permute-start = (bf16[2,256,2048]{1,2,0:T(8,128)(2,1)}, bf16[2,256,2048]{1,2,0:T(8,128)(2,1)}, u32[]{:S(2)}, u32[]{:S(2)}) collective-permute-start(bf16[2,256,2048]{1,2,0:T(8,128)(2,1)} %pad_maximum_fusion), channel_id=1, source_target_pairs={{0,1},{1,2},{2,3},{3,4},{4,5},{5,6},{6,7},{7,8},{8,9},{9,10},{10,1... | collective-permute-start | bytes 6291464 | tf_op jit(solution)/shard_map/ppermute | solution.py:18
  6.8 1.9 %copy.53 = bf16[16,2,2,128,128]{4,3,2,1,0:T(8,128)(2,1)} copy(bf16[16,2,2,128,128]{4,0,3,2,1:T(8,128)(2,1)S(1)} %maximum_bitcast_fusion) | data formatting | bytes 4194304 | tf_op jit(solution)/shard_map/reshape | solution.py:59
  8.8 6.6 %all-to-all-start = ((bf16[16,2,2,128,128]{4,3,2,1,0:T(8,128)(2,1)}), bf16[16,2,2,128,128]{4,3,2,1,0:T(8,128)(2,1)}, u32[]{:S(2)}, u32[]{:S(2)}) async-start(bf16[16,2,2,128,128]{4,3,2,1,0:T(8,128)(2,1)} %copy.53), calls=%async_computation | async-start | bytes 4194304 | tf_op jit(solution)/shard_map/all_to_all | solution.py:62
  15.4 51.1 %collective-permute-done = bf16[2,256,2048]{1,2,0:T(8,128)(2,1)} collective-permute-done((bf16[2,256,2048]{1,2,0:T(8,128)(2,1)}, bf16[2,256,2048]{1,2,0:T(8,128)(2,1)}, u32[]{:S(2)}, u32[]{:S(2)}) %collective-permute-start) | collective-permute-done | bytes 2097184 | tf_op jit(solution)/shard_map/ppermute | solution.py:18
  66.5 1.9 %collective-permute-start.1 = (bf16[2,256,2048]{1,2,0:T(8,128)(2,1)}, bf16[2,256,2048]{1,2,0:T(8,128)(2,1)}, u32[]{:S(2)}, u32[]{:S(2)}) collective-permute-start(bf16[2,256,2048]{1,2,0:T(8,128)(2,1)} %collective-permute-done), channel_id=1, source_target_pairs={{0,1},{1,2},{2,3},{3,4},{4,5},{5,6},{6,7},{7,8},{8,9},{9,10},{10,1... | collective-permute-start | bytes 6291464 | tf_op jit(solution)/shard_map/ppermute | solution.py:18
  69.5 30.8 %collective-permute-done.1 = bf16[2,256,2048]{1,2,0:T(8,128)(2,1)} collective-permute-done((bf16[2,256,2048]{1,2,0:T(8,128)(2,1)}, bf16[2,256,2048]{1,2,0:T(8,128)(2,1)}, u32[]{:S(2)}, u32[]{:S(2)}) %collective-permute-start.1) | collective-permute-done | bytes 2097184 | tf_op jit(solution)/shard_map/ppermute | solution.py:18
  100.3 1.9 %collective-permute-start.2 = (bf16[2,256,2048]{1,2,0:T(8,128)(2,1)}, bf16[2,256,2048]{1,2,0:T(8,128)(2,1)}, u32[]{:S(2)}, u32[]{:S(2)}) collective-permute-start(bf16[2,256,2048]{1,2,0:T(8,128)(2,1)} %collective-permute-done.1), channel_id=1, source_target_pairs={{0,1},{1,2},{2,3},{3,4},{4,5},{5,6},{6,7},{7,8},{8,9},{9,10},{10,1... | collective-permute-start | bytes 6291464 | tf_op jit(solution)/shard_map/ppermute | solution.py:18
  102.5 2.3 %copy.46 = bf16[256,2048]{0,1:T(8,128)(2,1)} copy(bf16[256,2048]{1,0:T(8,128)(2,1)} %param.9) | data formatting | bytes 2097152 | tf_op args[0]
  105.0 3.2 %copy.54 = bf16[16,2,2,128,128]{4,3,2,0,1:T(8,128)(2,1)} copy(bf16[16,2,2,128,128]{4,3,2,1,0:T(8,128)(2,1)} %all-to-all-done) | data formatting | bytes 4194304 | tf_op jit(solution)/shard_map/all_to_all | solution.py:62
  108.3 3.7 %gather_fusion = bf16[32,2,128,128]{3,2,1,0:T(8,128)(2,1)} fusion(bf16[2,32,128,128]{3,2,1,0:T(8,128)(2,1)} %bitcast.87, s32[1024]{0:T(1024)S(1)} %pad_clamp_fusion), kind=kCustom, calls=%fused_computation | custom fusion | bytes 4194432 | tf_op jit(solution)/shard_map/jit(_take)/gather | solution.py:63
  112.0 1.8 select_bitcast_fusion
  113.9 1.5 slice_bitcast_fusion
  115.3 13.6 %collective-permute-done.2 = bf16[2,256,2048]{1,2,0:T(8,128)(2,1)} collective-permute-done((bf16[2,256,2048]{1,2,0:T(8,128)(2,1)}, bf16[2,256,2048]{1,2,0:T(8,128)(2,1)}, u32[]{:S(2)}, u32[]{:S(2)}) %collective-permute-start.2) | collective-permute-done | bytes 2097184 | tf_op jit(solution)/shard_map/ppermute | solution.py:18
  128.9 3.9 %maximum_maximum_fusion = bf16[2,1024,2048]{1,2,0:T(8,128)(2,1)S(1)} fusion(bf16[1,256,2048]{1,2,0:T(8,128)(2,1)S(1)} %bitcast.86, bf16[1,256,2048]{1,2,0:T(8,128)(2,1)S(1)} %bitcast.84, bf16[2,256,2048]{1,2,0:T(8,128)(2,1)} %collective-permute-done, bf16[2,256,2048]{1,2,0:T(8,128)(2,1)} %collective-permute-done.1, ...), kind=kLoop, calls=%fused_computation.22 | loop fusion | flops 41943040 | bytes 16777216 | tf_op jit(solution)/shard_map/concatenate | solution.py:76
  132.8 3.7 %fusion.26 = (bf16[1,1024,2048]{1,2,0:T(8,128)(2,1)}, bf16[1,1024,2048]{1,2,0:T(8,128)(2,1)}) fusion(bf16[2,1024,2048]{1,2,0:T(8,128)(2,1)S(1)} %maximum_maximum_fusion), kind=kLoop, calls=%fused_computation.69 | loop fusion | bytes 16777216 | tf_op jit(solution)/shard_map/slice | solution.py:101
  136.4 51.3 %while.11 = (s32[]{:T(128)}, bf16[16,256,128]{2,1,0:T(8,128)(2,1)S(1)}, bf16[16,256,128]{1,2,0:T(8,128)(2,1)}, bf16[16,1024,128]{1,2,0:T(8,128)(2,1)}, bf16[16,1...) while((s32[]{:T(128)}, ...), condition=%wide.region_9.10_spmd.clone, body=%wide.region_6.0_spmd.clone.sunk | while | flops 137133568 | bytes 3884133 | solution.py:118
  136.4 1.5 fusion.35
  138.3 1.3 fusion.37
  139.6 1.5 fusion.35
  141.5 1.3 fusion.37
  142.9 1.5 fusion.35
  144.7 1.3 fusion.37
  146.1 1.5 fusion.35
  147.9 1.3 fusion.37
  149.3 1.5 fusion.35
  151.1 1.3 fusion.37
  152.5 1.5 fusion.35
  154.3 1.3 fusion.37
  155.7 1.5 fusion.35
  157.5 1.3 fusion.37
  158.9 1.5 fusion.35
  160.8 1.3 fusion.37
  162.1 1.5 fusion.35
  164.0 1.3 fusion.37
  165.3 1.5 fusion.35
  167.2 1.3 fusion.37
  168.5 1.5 fusion.35
  170.4 1.3 fusion.37
  171.7 1.5 fusion.35
  173.6 1.3 fusion.37
  174.9 1.5 fusion.35
  176.8 1.3 fusion.37
  178.1 1.5 fusion.35
  180.0 1.3 fusion.37
  181.4 1.5 fusion.35
  184.6 1.5 fusion.35
  (62 shorter events, 11.5 us)
Async XLA Ops:
  0.6 1.6 copy-start.1
  2.8 3.4 %copy-start = (bf16[256,2048]{1,0:T(8,128)(2,1)S(1)}, bf16[256,2048]{1,0:T(8,128)(2,1)}, u32[]{:S(2)}) copy-start(bf16[256,2048]{1,0:T(8,128)(2,1)} %param.10) | copy-start | bytes 3145732
  4.2 62.3 %collective-permute-start = (bf16[2,256,2048]{1,2,0:T(8,128)(2,1)}, bf16[2,256,2048]{1,2,0:T(8,128)(2,1)}, u32[]{:S(2)}, u32[]{:S(2)}) collective-permute-start(bf16[2,256,2048]{1,2,0:T(8,128)(2,1)} %pad_maximum_fusion), channel_id=1, source_target_pairs={{0,1},{1,2},{2,3},{3,4},{4,5},{5,6},{6,7},{7,8},{8,9},{9,10},{10,1... | collective-permute-start | bytes 6291464 | tf_op jit(solution)/shard_map/ppermute | solution.py:18
  8.8 59.6 %copy-start.5 = (s32[8]{0:T(128)S(1)}, s32[8]{0:T(128)}, u32[]{:S(2)}) copy-start(s32[8]{0:T(128)} %param.12) | copy-start | bytes 100
  8.8 59.7 %copy-start.2 = (s32[16]{0:T(128)S(1)}, s32[16]{0:T(128)}, u32[]{:S(2)}) copy-start(s32[16]{0:T(128)} %param.14) | copy-start | bytes 196
  8.8 59.7 %copy-start.4 = (s32[16]{0:T(128)S(1)}, s32[16]{0:T(128)}, u32[]{:S(2)}) copy-start(s32[16]{0:T(128)} %param.13) | copy-start | bytes 196
  8.8 60.3 %copy-start.3 = (s32[8]{0:T(128)S(1)}, s32[8]{0:T(128)}, u32[]{:S(2)}) copy-start(s32[8]{0:T(128)} %param.15) | copy-start | bytes 100
  8.8 96.2 %all-to-all-start = ((bf16[16,2,2,128,128]{4,3,2,1,0:T(8,128)(2,1)}), bf16[16,2,2,128,128]{4,3,2,1,0:T(8,128)(2,1)}, u32[]{:S(2)}, u32[]{:S(2)}) async-start(bf16[16,2,2,128,128]{4,3,2,1,0:T(8,128)(2,1)} %copy.53), calls=%async_computation | async-start | bytes 4194304 | tf_op jit(solution)/shard_map/all_to_all | solution.py:62
  66.5 33.8 %collective-permute-start.1 = (bf16[2,256,2048]{1,2,0:T(8,128)(2,1)}, bf16[2,256,2048]{1,2,0:T(8,128)(2,1)}, u32[]{:S(2)}, u32[]{:S(2)}) collective-permute-start(bf16[2,256,2048]{1,2,0:T(8,128)(2,1)} %collective-permute-done), channel_id=1, source_target_pairs={{0,1},{1,2},{2,3},{3,4},{4,5},{5,6},{6,7},{7,8},{8,9},{9,10},{10,1... | collective-permute-start | bytes 6291464 | tf_op jit(solution)/shard_map/ppermute | solution.py:18
  100.3 28.6 %collective-permute-start.2 = (bf16[2,256,2048]{1,2,0:T(8,128)(2,1)}, bf16[2,256,2048]{1,2,0:T(8,128)(2,1)}, u32[]{:S(2)}, u32[]{:S(2)}) collective-permute-start(bf16[2,256,2048]{1,2,0:T(8,128)(2,1)} %collective-permute-done.1), channel_id=1, source_target_pairs={{0,1},{1,2},{2,3},{3,4},{4,5},{5,6},{6,7},{7,8},{8,9},{9,10},{10,1... | collective-permute-start | bytes 6291464 | tf_op jit(solution)/shard_map/ppermute | solution.py:18
where the time goes:
time: 190 us; the launch traced here: 189 us
  waiting for transfers between devices  95.5 us (50%)
  matrix products  46.1 us (24%)
  local copies, waits for them, and re-layouts  19.4 us (10%)
  other arithmetic  14.5 us (8%)
  starting transfers between devices  12.3 us (6%)
    ppermute x3, waiting for transfers between devices, shifted(): return lax.ppermute(block, axis, route)  95.5 us
    dot_general x16, matrix products, one_head(): jnp.einsum('qd,kd->qk', query_part, key_part, preferred_element_type=jnp....  24.7 us
    dot_general x16, matrix products, one_head(): jnp.dot(weights.astype(jnp.bfloat16), value_part, preferred_element_type=...  21.4 us
    all_to_all x1, starting transfers between devices, hand_off(): lax.all_to_all(outgoing, 'seq', split_axis=0, concat_axis=2, tiled=True)  6.57 us
    unnamed x18, local copies, waits for them, and re-layouts  6.28 us
    ppermute x3, starting transfers between devices, shifted(): return lax.ppermute(block, axis, route)  5.73 us
    reduce_sum x16, other arithmetic, one_head(): totals = jnp.sum(weights, axis=1, keepdims=True)  4.88 us
    concatenate x1, other arithmetic, attend(): window = jnp.concatenate(pieces, axis=1)  3.88 us
  transfers between devices with their start and end apart: 4, of which 3 were waited for; matrix products, arithmetic and copies ran while one was open for 9% of the time, Pallas kernels for 0%

commit v1 on v0

v1 whole, which is shorter than its diff:
```python
import jax
import jax.numpy as jnp
from jax import lax
from jax.experimental import pallas as pl
from jax.experimental.pallas import tpu as pltpu
from jax.sharding import PartitionSpec as P

HEADS = 16
HEAD_DIM = 128
BLOCK = 128
MAXB = 6


MASKED_SCORE = -1e30


HEADS_STEP = 2
CHUNK = 32


def sent(block, pairs):
    return lax.ppermute(block, "seq", pairs)


def block_tables(block_counts, last_tokens, pack_order, decode_slot, total_blocks, block):
    pair_count = block_counts.shape[0]
    prompts = 2 * pair_count
    prompt_ids = jnp.arange(prompts, dtype=jnp.int32)
    prompt_sizes = jnp.concatenate([block_counts, jnp.ones((pair_count,), jnp.int32)])
    picked = (pack_order[:, None] == prompt_ids[None, :]).astype(jnp.int32)
    packed_sizes = jnp.sum(picked * prompt_sizes[None, :], axis=1)
    packed_tails = jnp.sum(picked * last_tokens[None, :], axis=1)
    block_ends = jnp.cumsum(packed_sizes)
    starts = block_ends - packed_sizes
    blocks = jnp.arange(total_blocks, dtype=jnp.int32)
    member = (
        (starts[None, :] <= blocks[:, None]) & (blocks[:, None] < block_ends[None, :])
    ).astype(jnp.int32)
    prompt = jnp.sum(member * pack_order[None, :], axis=1)
    within = blocks - jnp.sum(member * starts[None, :], axis=1)
    is_last = blocks + 1 == jnp.sum(member * block_ends[None, :], axis=1)
    valid_tokens = jnp.where(is_last, jnp.sum(member * packed_tails[None, :], axis=1), block)
    pair_ids = jnp.arange(pair_count, dtype=jnp.int32)
    earlier = (decode_slot[None, :] < decode_slot[:, None]).astype(jnp.int32)
    slot_start = jnp.sum(earlier * (block_counts + 1)[None, :], axis=1)
    pair_of = prompt % pair_count
    owner = (pair_of[:, None] == pair_ids[None, :]).astype(jnp.int32)
    base_slot = jnp.sum(owner * slot_start[None, :], axis=1)
    own_count = jnp.sum(owner * block_counts[None, :], axis=1)
    destination = base_slot + jnp.where(prompt >= pair_count, own_count, within)
    hits = (destination[None, :] == blocks[:, None]).astype(jnp.int32)
    source = jnp.sum(hits * blocks[None, :], axis=1)
    return (within, valid_tokens, source)


def pack_kernel(keys, values, out):
    splits, _, blocks_here, slice_len, _ = out.shape
    for which, ref in enumerate((keys, values)):
        for b in range(blocks_here):
            for t in range(splits):
                first = b * BLOCK + t * slice_len
                out[t, which, b] = ref[first : first + slice_len, :]


def packed(keys, values, splits):
    tokens_here = keys.shape[0]
    blocks_here = tokens_here // BLOCK
    slice_len = BLOCK // splits
    piece = (splits, 2, blocks_here, slice_len, HEAD_DIM)
    spec = pl.BlockSpec((tokens_here, HEAD_DIM), lambda h: (0, h))
    return pl.pallas_call(
        pack_kernel,
        grid=(HEADS,),
        in_specs=[spec, spec],
        out_specs=pl.BlockSpec(piece, lambda h: (h, 0, 0, 0, 0)),
        out_shape=jax.ShapeDtypeStruct((HEADS * splits,) + piece[1:], keys.dtype),
    )(keys, values)


def order_kernel(source, arrived, cache_keys, cache_values, sems):
    blocks_here = arrived.shape[2]
    total = cache_keys.shape[1]
    wave = sems.shape[0]

    def copies(start, i):
        block = source[start + i]
        device = block // blocks_here
        local_block = block % blocks_here
        return [
            pltpu.make_async_copy(
                arrived.at[device, which, local_block], out.at[0, start + i], sems.at[i, which]
            )
            for which, out in enumerate((cache_keys, cache_values))
        ]

    def one_wave(step, carry):
        for i in range(wave):
            for copy in copies(step * wave, i):
                copy.start()
        for i in range(wave):
            for copy in copies(step * wave, i):
                copy.wait()
        return carry

    lax.fori_loop(0, total // wave, one_wave, 0)


def ordered(arrived, source):
    total = source.shape[0]
    wave = min(CHUNK, total)
    shape = jax.ShapeDtypeStruct((1, total) + arrived.shape[3:], arrived.dtype)
    anywhere = pl.BlockSpec(memory_space=pl.ANY)
    return pl.pallas_call(
        order_kernel,
        grid_spec=pltpu.PrefetchScalarGridSpec(
            num_scalar_prefetch=1,
            grid=(1,),
            in_specs=[anywhere],
            out_specs=[anywhere, anywhere],
            scratch_shapes=[pltpu.SemaphoreType.DMA((wave, 2))],
        ),
        out_shape=[shape, shape],
    )(source, arrived)


def attend_kernel(info, q, *refs):
    key_refs, value_refs, out = refs[:5], refs[5:10], refs[10]
    odd = info[0] == 1

    def block_of(group, index, lanes):
        far, two, swapped, near, own = group
        lo, hi = slice(0, BLOCK), slice(BLOCK, 2 * BLOCK)
        rows = hi if index % 2 == 0 else lo
        if index == 0:
            return jnp.where(odd, swapped[hi, lanes], far[:, lanes])
        if index <= 2:
            return two[rows, lanes]
        if index <= 4:
            return jnp.where(odd, near[rows, lanes], swapped[rows, lanes])
        return own[rows, lanes]

    row = lax.broadcasted_iota(jnp.int32, (BLOCK, BLOCK), 0)
    col = lax.broadcasted_iota(jnp.int32, (BLOCK, BLOCK), 1)
    scale = HEAD_DIM ** (-0.5) * 1.4426950408889634

    def one(head, query_block, prior):
        lanes = slice(head * HEAD_DIM, (head + 1) * HEAD_DIM)
        rows = slice(query_block * BLOCK, (query_block + 1) * BLOCK)
        last = MAXB - 1 + query_block
        valid = info[3 + query_block]
        query = q[rows, lanes]
        window = range(last - prior, last + 1)
        parts = [
            lax.dot_general(
                query,
                block_of(key_refs, j, lanes),
                (((1,), (1,)), ((), ())),
                preferred_element_type=jnp.float32,
            )
            for j in window
        ]
        parts[-1] = jnp.where((col <= row) & (col < valid), parts[-1], MASKED_SCORE)
        best = parts[0]
        for part in parts[1:]:
            best = jnp.maximum(best, part)
        peak = jnp.max(best, axis=1, keepdims=True)
        weights = [jnp.exp2((part - peak) * scale) for part in parts]
        summed = weights[0]
        for part in weights[1:]:
            summed = summed + part
        totals = jnp.sum(summed, axis=1, keepdims=True)
        mixed = jnp.zeros((BLOCK, HEAD_DIM), jnp.float32)
        for j, part in zip(window, weights):
            mixed = mixed + jnp.dot(
                part.astype(jnp.bfloat16),
                block_of(value_refs, j, lanes),
                preferred_element_type=jnp.float32,
            )
        result = jnp.where(row < valid, mixed / totals, 0.0)
        out[rows, lanes] = result.astype(jnp.bfloat16)

    for query_block in range(2):
        for prior in range(MAXB):

            @pl.when(info[1 + query_block] == prior)
            def _():
                for head in range(HEADS_STEP):
                    one(head, query_block, prior)


def attend(info, queries, key_parts, value_parts):
    width = HEADS_STEP * HEAD_DIM
    tokens_here, features = queries.shape
    half = tokens_here // 2
    whole = pl.BlockSpec((tokens_here, width), lambda h, info: (0, h))
    far = pl.BlockSpec((half, width), lambda h, info: (0, h * (1 - info[0])))
    near = pl.BlockSpec((tokens_here, width), lambda h, info: (0, h * info[0]))
    group = [far, whole, whole, near, whole]
    return pl.pallas_call(
        attend_kernel,
        grid_spec=pltpu.PrefetchScalarGridSpec(
            num_scalar_prefetch=1,
            grid=(features // width,),
            in_specs=[whole] + group + group,
            out_specs=whole,
        ),
        out_shape=jax.ShapeDtypeStruct(queries.shape, jnp.bfloat16),
        cost_estimate=pl.CostEstimate(
            flops=4 * tokens_here * MAXB * BLOCK * features,
            transcendentals=0,
            bytes_accessed=10 * tokens_here * features,
        ),
    )(info, queries, *key_parts, *value_parts)


def window_parts(own, devices):
    by_two = [(i, i + 2) for i in range(devices - 2)]
    by_three = [(i, i + 3) for i in range(1, devices - 3, 2)]
    to_odd = [(i, i + 1) for i in range(0, devices, 2)]
    exchange = [(i, i ^ 1) for i in range(devices)]
    two = sent(own, by_two)
    far = sent(own[BLOCK:], by_three)
    near = sent(own, to_odd)
    swapped = sent(two, exchange)
    return [far, two, swapped, near, own]


def local(queries, keys, values, block_counts, last_tokens, pack_order, decode_slot):
    devices = lax.axis_size("seq")
    own_index = lax.axis_index("seq")
    blocks_here = queries.shape[0] // BLOCK
    assert blocks_here == 2 and devices % 2 == 0
    splits = devices // HEADS
    within, valid_tokens, source = block_tables(
        block_counts, last_tokens, pack_order, decode_slot, blocks_here * devices, BLOCK
    )
    key_parts = window_parts(keys, devices)
    value_parts = window_parts(values, devices)
    arrived = lax.all_to_all(
        packed(keys, values, splits), "seq", split_axis=0, concat_axis=0, tiled=True
    )
    first = own_index * blocks_here
    info = jnp.concatenate(
        [
            (own_index % 2)[None].astype(jnp.int32),
            lax.dynamic_slice_in_dim(within, first, blocks_here),
            lax.dynamic_slice_in_dim(valid_tokens, first, blocks_here),
        ]
    )
    attended = attend(info, queries, key_parts, value_parts)
    cache_keys, cache_values = ordered(arrived, source)
    return (attended, cache_keys, cache_values)


def solution(mesh):
    placed = (
        P(("groups", "seq"), None),
        P(("groups", "seq"), None),
        P(("groups", "seq"), None),
        P("groups"),
        P("groups"),
        P("groups"),
        P("groups"),
    )
    return jax.shard_map(
        local,
        mesh=mesh,
        in_specs=placed,
        out_specs=(
            P(("groups", "seq"), None),
            P(("groups", "seq"), None, None, None),
            P(("groups", "seq"), None, None, None),
        ),
        check_vma=False,
    )
```

time: 190 us -> 207 us (1.089)
  Pallas kernels: 0 us -> 90.7 us
  matrix products: 46.1 us -> 0 us
  local copies, waits for them, and re-layouts: 19.4 us -> 4.33 us
  other arithmetic: 14.5 us -> 2.06 us
  waiting for transfers between devices: 95.5 us -> 86.6 us
  starting transfers between devices: 12.3 us -> 20.3 us
    pallas_call x0 -> x3, Pallas kernels: none -> 90.7 us  [the longest x1 65.9 us: ordered(): pl.pallas_call(order_kernel, grid_spec=pltpu.PrefetchScalarGridSpec(num_s...]
    dot_general x32 -> x0, matrix products: 46.1 us -> none  [the longest x16 24.7 us: one_head(): jnp.einsum('qd,kd->qk', query_part, key_part, preferred_element_type=jnp....]
    ppermute x3 -> x8, waiting for transfers between devices: 95.5 us -> 86.6 us  [sent(): return lax.ppermute(block, 'seq', pairs)]
    ppermute x3 -> x8, starting transfers between devices: 5.73 us -> 14 us  [sent(): return lax.ppermute(block, 'seq', pairs)]
    unnamed x18 -> x12, local copies, waits for them, and re-layouts: 6.28 us -> 1.37 us
    reduce_sum x18 -> x2, other arithmetic: 5.16 us -> 0.27 us  [the longest x1 0.18 us: block_tables(): packed_sizes = jnp.sum(picked * prompt_sizes[None, :], axis=1)]
    gather x1 -> x0, local copies, waits for them, and re-layouts: 3.75 us -> none  [hand_off(): ordered = jnp.take(arrived[0], source, axis=1)]
    all_to_all x1 -> x0, local copies, waits for them, and re-layouts: 3.23 us -> none  [hand_off(): lax.all_to_all(outgoing, 'seq', split_axis=0, concat_axis=2, tiled=True)]
  transfers between devices with their start and end apart: 4 -> 9, of which waited for: 3 -> 3; matrix products, arithmetic and copies ran while one was open for 9% -> 2% of each run, Pallas kernels for 0% -> 8%
where the time goes in v1:
time: 207 us; the launch traced here: 205 us
  Pallas kernels  90.7 us (44%)
  waiting for transfers between devices  86.6 us (42%)
  starting transfers between devices  20.3 us (10%)
  local copies, waits for them, and re-layouts  4.33 us (2%)
    ppermute x8, waiting for transfers between devices, sent(): return lax.ppermute(block, 'seq', pairs)  86.6 us
    pallas_call x1, Pallas kernels, ordered(): pl.pallas_call(order_kernel, grid_spec=pltpu.PrefetchScalarGridSpec(num_s...  65.9 us
    pallas_call x1, Pallas kernels, attend(): pl.pallas_call(attend_kernel, grid_spec=pltpu.PrefetchScalarGridSpec(num_...  15.6 us
    ppermute x8, starting transfers between devices, sent(): return lax.ppermute(block, 'seq', pairs)  14 us
    pallas_call x1, Pallas kernels, packed(): pl.pallas_call(pack_kernel, grid=(HEADS,), in_specs=[spec, spec], out_spe...  9.25 us
    all_to_all x1, starting transfers between devices, local(): lax.all_to_all(packed(keys, values, splits), 'seq', split_axis=0, concat_...  6.3 us
  transfers between devices with their start and end apart: 9, of which 3 were waited for; matrix products, arithmetic and copies ran while one was open for 2% of the time, Pallas kernels for 8%

profile of v1, /device:TPU:20, one launch (start us, length us, event | category | flops | bytes accessed | tf_op | source)
XLA Modules:
  0.0 204.8 jit_solution(15718897274376255812)
XLA Ops:
  0.6 9.3 %shard_map.95 = bf16[16,2,2,128,128]{4,3,2,1,0:T(8,128)(2,1)} custom-call(bf16[256,2048]{1,0:T(8,128)(2,1)} %keys.1, bf16[256,2048]{1,0:T(8,128)(2,1)} %values.1), custom_call_target="tpu_custom_call" | custom-call | tf_op jit(solution)/shard_map/pallas_call | solution.py:71
  9.9 0.0 copy-start.1
  9.9 0.0 copy-start.5
  9.9 0.0 copy-start.3
  9.9 0.0 copy-start.4
  9.9 6.3 %all-to-all-start = ((bf16[16,2,2,128,128]{4,3,2,1,0:T(8,128)(2,1)}), bf16[16,2,2,128,128]{4,3,2,1,0:T(8,128)(2,1)S(1)}, u32[]{:S(2)}, u32[]{:S(2)}) async-start(bf16[16,2,2,128,128]{4,3,2,1,0:T(8,128)(2,1)} %shard_map.95), calls=%async_computation | async-start | bytes 4194304 | tf_op jit(solution)/shard_map/all_to_all | solution.py:239
  16.2 0.0 copy-done.1
  16.2 0.0 copy-start.2
  16.2 3.4 %collective-permute-start.1 = (bf16[256,2048]{1,0:T(8,128)(2,1)S(1)}, bf16[256,2048]{1,0:T(8,128)(2,1)}, u32[]{:S(2)}, u32[]{:S(2)}) collective-permute-start(bf16[256,2048]{1,0:T(8,128)(2,1)S(1)} %copy-done.1), channel_id=1, source_target_pairs={{0,2},{1,3},{2,4},{3,5},{4,6},{5,7},{6,8},{7,9},{8,10},{9,11},{10,... | collective-permute-start | bytes 3145736 | tf_op jit(solution)/shard_map/ppermute | solution.py:22
  19.6 3.4 %collective-permute-start.5 = (bf16[256,2048]{1,0:T(8,128)(2,1)}, bf16[256,2048]{1,0:T(8,128)(2,1)}, u32[]{:S(2)}, u32[]{:S(2)}) collective-permute-start(bf16[256,2048]{1,0:T(8,128)(2,1)} %values.1), channel_id=1, source_target_pairs={{0,2},{1,3},{2,4},{3,5},{4,6},{5,7},{6,8},{7,9},{8,10},{9,11},{10,... | collective-permute-start | bytes 3145736 | tf_op jit(solution)/shard_map/ppermute | solution.py:22
  23.0 2.4 %collective-permute-start.3 = (bf16[256,2048]{1,0:T(8,128)(2,1)S(1)}, bf16[256,2048]{1,0:T(8,128)(2,1)}, u32[]{:S(2)}, u32[]{:S(2)}) collective-permute-start(bf16[256,2048]{1,0:T(8,128)(2,1)S(1)} %copy-done.1), channel_id=1, source_target_pairs={{0,1},{2,3},{4,5},{6,7},{8,9},{10,11},{12,13},{14,15},{16,17},{18,... | collective-permute-start | bytes 3145736 | tf_op jit(solution)/shard_map/ppermute | solution.py:22
  25.4 2.3 %collective-permute-start.7 = (bf16[256,2048]{1,0:T(8,128)(2,1)}, bf16[256,2048]{1,0:T(8,128)(2,1)}, u32[]{:S(2)}, u32[]{:S(2)}) collective-permute-start(bf16[256,2048]{1,0:T(8,128)(2,1)} %values.1), channel_id=1, source_target_pairs={{0,1},{2,3},{4,5},{6,7},{8,9},{10,11},{12,13},{14,15},{16,17},{18,... | collective-permute-start | bytes 3145736 | tf_op jit(solution)/shard_map/ppermute | solution.py:22
  27.7 1.9 slice.7
  29.6 1.3 collective-permute-start.4
  30.9 0.0 copy-done.5
  30.9 56.2 %collective-permute-done.1.refs_1_ = bf16[256,2048]{1,0:T(8,128)(2,1)} collective-permute-done((bf16[256,2048]{1,0:T(8,128)(2,1)S(1)}, bf16[256,2048]{1,0:T(8,128)(2,1)}, u32[]{:S(2)}, u32[]{:S(2)}) %collective-permute-start.1) | collective-permute-done | bytes 1048608 | tf_op jit(solution)/shard_map/ppermute | solution.py:22
  87.1 0.0 collective-permute-start.2
  87.1 22.5 %collective-permute-done.5.refs_6_ = bf16[256,2048]{1,0:T(8,128)(2,1)} collective-permute-done((bf16[256,2048]{1,0:T(8,128)(2,1)}, bf16[256,2048]{1,0:T(8,128)(2,1)}, u32[]{:S(2)}, u32[]{:S(2)}) %collective-permute-start.5) | collective-permute-done | bytes 1048608 | tf_op jit(solution)/shard_map/ppermute | solution.py:22
  109.5 0.0 collective-permute-start.6
  109.5 0.0 copy-done.3
  109.5 0.0 copy-done.4
  109.5 0.2 select_reduce_fusion.6
  109.7 0.8 slice.6
  110.6 0.1 copy.12
  110.7 0.1 reduce
  110.8 0.0 copy-done.2
  110.8 0.2 select_reduce_fusion.9
  111.0 0.1 select_reduce_fusion.1
  111.1 0.0 collective-permute-done.4.refs_5_
  111.1 1.3 collective-permute-start
  112.4 0.1 select_reduce_fusion.7
  112.5 0.1 dynamic_slice.6
  112.6 0.1 dynamic_slice.7
  112.7 0.7 pad_add_fusion.info
  113.3 0.7 select_reduce_fusion.source
  114.0 7.9 %collective-permute-done.refs_0_ = bf16[128,2048]{1,0:T(8,128)(2,1)} collective-permute-done((bf16[128,2048]{1,0:T(8,128)(2,1)}, bf16[128,2048]{1,0:T(8,128)(2,1)}, u32[]{:S(2)}, u32[]{:S(2)}) %collective-permute-start) | collective-permute-done | bytes 524320 | tf_op jit(solution)/shard_map/ppermute | solution.py:22
  121.9 0.0 collective-permute-done.3.refs_3_
  121.9 0.0 collective-permute-done.7.refs_8_
  121.9 0.0 collective-permute-done.2.refs_2_
  121.9 0.0 collective-permute-done.6.refs_7_
  122.0 15.6 %shard_map.94 = bf16[256,2048]{1,0:T(8,128)(2,1)} custom-call(s32[5]{0:T(128)} %pad_add_fusion.info, bf16[256,2048]{1,0:T(8,128)(2,1)} %q.1, bf16[128,2048]{1,0:T(8,128)(2,1)} %collective-permute-done.refs_0_, bf16[256,2048]{1,0:T(8,128)(2,1)} %collective-permute-done.1.refs_1_, bf16[256,2048]{1,0:T(8,128)(2,1)} %collective-permute-done.2.refs_2_, ...), custom_call_target="tpu_custom_call" | custom-call | flops 1610612736 | bytes 5242880 | tf_op jit(solution)/shard_map/pallas_call | solution.py:199
  137.5 0.0 all-to-all-done.arrived
  137.5 0.0 copy-start
  137.5 1.3 copy-done
  138.9 65.9 %shard_map.96 = (bf16[1,32,128,128]{3,2,1,0:T(8,128)(2,1)}, bf16[1,32,128,128]{3,2,1,0:T(8,128)(2,1)}) custom-call(s32[32]{0:T(128)} %select_reduce_fusion.source, bf16[16,2,2,128,128]{4,3,2,1,0:T(8,128)(2,1)} %copy-done), custom_call_target="tpu_custom_call" | custom-call | tf_op jit(solution)/shard_map/pallas_call | solution.py:113
  (6 shorter events, 0.1 us)
Async XLA Ops:
  9.9 6.3 %copy-start.1 = (bf16[256,2048]{1,0:T(8,128)(2,1)S(1)}, bf16[256,2048]{1,0:T(8,128)(2,1)}, u32[]{:S(2)}) copy-start(bf16[256,2048]{1,0:T(8,128)(2,1)} %keys.1) | copy-start | bytes 3145732
  9.9 21.0 %copy-start.5 = (s32[8]{0:T(128)S(1)}, s32[8]{0:T(128)}, u32[]{:S(2)}) copy-start(s32[8]{0:T(128)} %param.10) | copy-start | bytes 100
  9.9 99.6 %copy-start.3 = (s32[16]{0:T(128)S(1)}, s32[16]{0:T(128)}, u32[]{:S(2)}) copy-start(s32[16]{0:T(128)} %param.12) | copy-start | bytes 196
  9.9 99.6 %copy-start.4 = (s32[16]{0:T(128)S(1)}, s32[16]{0:T(128)}, u32[]{:S(2)}) copy-start(s32[16]{0:T(128)} %param.11) | copy-start | bytes 196
  9.9 127.6 %all-to-all-start = ((bf16[16,2,2,128,128]{4,3,2,1,0:T(8,128)(2,1)}), bf16[16,2,2,128,128]{4,3,2,1,0:T(8,128)(2,1)S(1)}, u32[]{:S(2)}, u32[]{:S(2)}) async-start(bf16[16,2,2,128,128]{4,3,2,1,0:T(8,128)(2,1)} %shard_map.95), calls=%async_computation | async-start | bytes 4194304 | tf_op jit(solution)/shard_map/all_to_all | solution.py:239
  16.2 94.6 %copy-start.2 = (s32[8]{0:T(128)S(1)}, s32[8]{0:T(128)}, u32[]{:S(2)}) copy-start(s32[8]{0:T(128)} %param.13) | copy-start | bytes 100
  16.2 70.8 %collective-permute-start.1 = (bf16[256,2048]{1,0:T(8,128)(2,1)S(1)}, bf16[256,2048]{1,0:T(8,128)(2,1)}, u32[]{:S(2)}, u32[]{:S(2)}) collective-permute-start(bf16[256,2048]{1,0:T(8,128)(2,1)S(1)} %copy-done.1), channel_id=1, source_target_pairs={{0,2},{1,3},{2,4},{3,5},{4,6},{5,7},{6,8},{7,9},{8,10},{9,11},{10,... | collective-permute-start | bytes 3145736 | tf_op jit(solution)/shard_map/ppermute | solution.py:22
  19.6 89.9 %collective-permute-start.5 = (bf16[256,2048]{1,0:T(8,128)(2,1)}, bf16[256,2048]{1,0:T(8,128)(2,1)}, u32[]{:S(2)}, u32[]{:S(2)}) collective-permute-start(bf16[256,2048]{1,0:T(8,128)(2,1)} %values.1), channel_id=1, source_target_pairs={{0,2},{1,3},{2,4},{3,5},{4,6},{5,7},{6,8},{7,9},{8,10},{9,11},{10,... | collective-permute-start | bytes 3145736 | tf_op jit(solution)/shard_map/ppermute | solution.py:22
  23.0 99.0 %collective-permute-start.3 = (bf16[256,2048]{1,0:T(8,128)(2,1)S(1)}, bf16[256,2048]{1,0:T(8,128)(2,1)}, u32[]{:S(2)}, u32[]{:S(2)}) collective-permute-start(bf16[256,2048]{1,0:T(8,128)(2,1)S(1)} %copy-done.1), channel_id=1, source_target_pairs={{0,1},{2,3},{4,5},{6,7},{8,9},{10,11},{12,13},{14,15},{16,17},{18,... | collective-permute-start | bytes 3145736 | tf_op jit(solution)/shard_map/ppermute | solution.py:22
  25.4 96.5 %collective-permute-start.7 = (bf16[256,2048]{1,0:T(8,128)(2,1)}, bf16[256,2048]{1,0:T(8,128)(2,1)}, u32[]{:S(2)}, u32[]{:S(2)}) collective-permute-start(bf16[256,2048]{1,0:T(8,128)(2,1)} %values.1), channel_id=1, source_target_pairs={{0,1},{2,3},{4,5},{6,7},{8,9},{10,11},{12,13},{14,15},{16,17},{18,... | collective-permute-start | bytes 3145736 | tf_op jit(solution)/shard_map/ppermute | solution.py:22
  29.6 81.5 %collective-permute-start.4 = (bf16[128,2048]{1,0:T(8,128)(2,1)}, bf16[128,2048]{1,0:T(8,128)(2,1)}, u32[]{:S(2)}, u32[]{:S(2)}) collective-permute-start(bf16[128,2048]{1,0:T(8,128)(2,1)} %slice.7), channel_id=1, source_target_pairs={{1,4},{3,6},{5,8},{7,10},{9,12},{11,14},{17,20},{19,22},{21,24},{2... | collective-permute-start | bytes 1572872 | tf_op jit(solution)/shard_map/ppermute | solution.py:22
  87.1 34.9 %collective-permute-start.2 = (bf16[256,2048]{1,0:T(8,128)(2,1)}, bf16[256,2048]{1,0:T(8,128)(2,1)}, u32[]{:S(2)}, u32[]{:S(2)}) collective-permute-start(bf16[256,2048]{1,0:T(8,128)(2,1)} %collective-permute-done.1.refs_1_), channel_id=1, source_target_pairs={{0,1},{1,0},{2,3},{3,2},{4,5},{5,4},{6,7},{7,6},{8,9},{9,8},{10,11... | collective-permute-start | bytes 3145736 | tf_op jit(solution)/shard_map/ppermute | solution.py:22
  109.5 12.4 %collective-permute-start.6 = (bf16[256,2048]{1,0:T(8,128)(2,1)}, bf16[256,2048]{1,0:T(8,128)(2,1)}, u32[]{:S(2)}, u32[]{:S(2)}) collective-permute-start(bf16[256,2048]{1,0:T(8,128)(2,1)} %collective-permute-done.5.refs_6_), channel_id=1, source_target_pairs={{0,1},{1,0},{2,3},{3,2},{4,5},{5,4},{6,7},{7,6},{8,9},{9,8},{10,11... | collective-permute-start | bytes 3145736 | tf_op jit(solution)/shard_map/ppermute | solution.py:22
  111.1 10.8 %collective-permute-start = (bf16[128,2048]{1,0:T(8,128)(2,1)}, bf16[128,2048]{1,0:T(8,128)(2,1)}, u32[]{:S(2)}, u32[]{:S(2)}) collective-permute-start(bf16[128,2048]{1,0:T(8,128)(2,1)} %slice.6), channel_id=1, source_target_pairs={{1,4},{3,6},{5,8},{7,10},{9,12},{11,14},{17,20},{19,22},{21,24},{2... | collective-permute-start | bytes 1572872 | tf_op jit(solution)/shard_map/ppermute | solution.py:22
  137.5 1.4 copy-start
